TPU v7x, 32 devices: a whole 2x2x4 slice. The times are simulated.
32 devices in a mesh: gx: 2 (over core), gy: 16 (over z, y, x).
Axes of the slice: x: 2, y: 2, z: 4, core: 2. Of those that a mesh axis runs over, the one named last changes fastest.
Arguments:
- right_side: float32 [128, 4096], P('gx', 'gy'), may hold values from -34 to 34, as said below
- initial: float32 [128, 4096], P('gx', 'gy'), may hold values from -0.6 to 0.6
- reaction: float32 [128, 4096], P('gx', 'gy'), may hold values from 0.05 to 0.5
- velocity_x: float32 [128, 4096], P('gx', 'gy'), may hold values from -1 to 1
- velocity_y: float32 [128, 4096], P('gx', 'gy'), may hold values from -1 to 1
Outputs:
- solution: float32 [128, 4096], P('gx', 'gy')
- residual: float32 [128, 4096], P('gx', 'gy')
Inputs may be any that keep to these rules, and one draw needn't show every extreme that they name: right_side is noise bounded by 4 in size times an envelope 0.5 + 8 g, where g is a periodic Gaussian bump of one device block's width along each dimension centred at a drawn position, so its entries lie within -34 and 34.
All inputs are finite; a program needn't handle non-finite values.
Results may differ from a plain program's by a relative error of at most 0.0075.
Values sent between devices are 32-bit elements.
A program may use at most 64 MiB of HBM per device.

v0:
```python
import jax
import jax.numpy as jnp
from jax import lax
from jax.sharding import PartitionSpec as P

RESTART = 15


def padded_2(cells, sides, width, closed):
    for axis, dim in sides:
        count = lax.axis_size(axis)
        ends = count if closed else count - 1
        head = lax.slice_in_dim(cells, 0, width, axis=dim)
        tail = lax.slice_in_dim(cells, cells.shape[dim] - width, cells.shape[dim], axis=dim)
        cells = jnp.concatenate(
            [
                lax.ppermute(tail, axis, [(i, (i + 1) % count) for i in range(ends)]),
                cells,
                lax.ppermute(head, axis, [((i + 1) % count, i) for i in range(ends)]),
            ],
            axis=dim,
        )
    return cells


def shifted(padded, offset, dimension, extent):
    row_start = 2 + offset if dimension == 0 else 2
    column_start = 2 + offset if dimension == 1 else 2
    return lax.slice(
        padded, (row_start, column_start), (row_start + extent[0], column_start + extent[1])
    )


def first_diff(padded, dimension, extent):
    outer = shifted(padded, -2, dimension, extent) - shifted(padded, 2, dimension, extent)
    inner = shifted(padded, 1, dimension, extent) - shifted(padded, -1, dimension, extent)
    return (outer + 8.0 * inner) / 12.0


def second_diff(padded, dimension, extent):
    inner = shifted(padded, 1, dimension, extent) + shifted(padded, -1, dimension, extent)
    outer = shifted(padded, 2, dimension, extent) + shifted(padded, -2, dimension, extent)
    return (16.0 * inner - outer - 30.0 * shifted(padded, 0, dimension, extent)) / 12.0


def apply_operator(field, padded_field, padded_speeds, reaction, velocity_x, velocity_y):
    extent = field.shape
    diffusion = second_diff(padded_field, 0, extent) + second_diff(padded_field, 1, extent)
    advect_x = 0.5 * (
        velocity_x * first_diff(padded_field, 0, extent)
        + first_diff(padded_speeds[0] * padded_field, 0, extent)
    )
    advect_y = 0.5 * (
        velocity_y * first_diff(padded_field, 1, extent)
        + first_diff(padded_speeds[1] * padded_field, 1, extent)
    )
    return reaction * field - diffusion + advect_x + advect_y


def least_squares(hessenberg, beta):
    columns_total = hessenberg.shape[1]
    target = jnp.where(jnp.arange(columns_total + 1) == 0, beta, 0.0)

    def rotate(column, carried):
        upper, target = carried
        top_row = upper[column]
        next_row = upper[column + 1]
        diagonal_entry = top_row[column]
        below_entry = next_row[column]
        radius = jnp.sqrt(diagonal_entry * diagonal_entry + below_entry * below_entry)
        cosine = diagonal_entry / radius
        sine_value = below_entry / radius
        upper = upper.at[column].set(cosine * top_row + sine_value * next_row)
        upper = upper.at[column + 1].set(cosine * next_row - sine_value * top_row)
        upper_value = target[column]
        lower_value = target[column + 1]
        target = target.at[column].set(cosine * upper_value + sine_value * lower_value)
        target = target.at[column + 1].set(cosine * lower_value - sine_value * upper_value)
        return (upper, target)

    upper, target = lax.fori_loop(0, columns_total, rotate, (hessenberg, target))

    def substitute(count, weights):
        row_index = columns_total - 1 - count
        known = jnp.sum(upper[row_index] * weights)
        return weights.at[row_index].set((target[row_index] - known) / upper[row_index, row_index])

    return lax.fori_loop(0, columns_total, substitute, jnp.zeros((columns_total,), jnp.float32))


def shards(right_side, initial, reaction, velocity_x, velocity_y):
    row_count, column_count = right_side.shape
    speeds = jnp.stack([velocity_x, velocity_y])
    padded_speeds = padded_2(speeds, (("gx", 1), ("gy", 2)), 2, True)

    def operator_on(field):
        padded_field = padded_2(field, (("gx", 0), ("gy", 1)), 2, True)
        return apply_operator(field, padded_field, padded_speeds, reaction, velocity_x, velocity_y)

    start_residual = right_side - operator_on(initial)
    start_square = lax.psum(jnp.sum(start_residual * start_residual), ("gx", "gy"))
    beta = jnp.sqrt(start_square)
    basis = jnp.zeros((RESTART + 1, row_count, column_count), jnp.float32)
    basis = basis.at[0].set(start_residual / beta)
    hessenberg = jnp.zeros((RESTART + 1, RESTART), jnp.float32)
    positions = jnp.arange(RESTART + 1)

    def arnoldi(column, carried):
        basis, hessenberg = carried
        current = lax.dynamic_index_in_dim(basis, column, 0, keepdims=False)
        applied = operator_on(current)
        local_projection = jnp.einsum("kxy,xy->k", basis, applied, precision=lax.Precision.HIGHEST)
        projection, applied_square = lax.psum(
            (local_projection, jnp.sum(applied * applied)), ("gx", "gy")
        )
        applied = applied - jnp.einsum(
            "k,kxy->xy", projection, basis, precision=lax.Precision.HIGHEST
        )
        length = jnp.sqrt(applied_square - jnp.sum(projection * projection))
        entries = jnp.where(positions == column + 1, length, projection)
        hessenberg = lax.dynamic_update_slice(hessenberg, entries[:, None], (0, column))
        basis = lax.dynamic_update_index_in_dim(basis, applied / length, column + 1, 0)
        return (basis, hessenberg)

    basis, hessenberg = lax.fori_loop(0, RESTART, arnoldi, (basis, hessenberg))
    weights = least_squares(hessenberg, beta)
    padded_weights = jnp.concatenate([weights, jnp.zeros((1,), jnp.float32)])
    solution = initial + jnp.einsum(
        "k,kxy->xy", padded_weights, basis, precision=lax.Precision.HIGHEST
    )
    padded_solution = padded_2(solution, (("gx", 0), ("gy", 1)), 2, True)
    residual = right_side - apply_operator(
        solution, padded_solution, padded_speeds, reaction, velocity_x, velocity_y
    )
    return (solution, residual)


def solution(mesh):
    return jax.shard_map(
        shards,
        mesh=mesh,
        in_specs=(P("gx", "gy"), P("gx", "gy"), P("gx", "gy"), P("gx", "gy"), P("gx", "gy")),
        out_specs=(P("gx", "gy"), P("gx", "gy")),
        check_vma=False,
    )
```

profile of v0, /device:TPU:0, one launch (start us, length us, event | category | flops | bytes accessed | tf_op | source)
XLA Modules:
  0.0 1141.1 jit_solution(10870514458512351832)
XLA Ops:
  3.7 6.6 collective-permute-start.6
  10.6 5.7 collective-permute-start.11
  22.2 38.4 %psum.35 = f32[]{:T(128)} all-reduce(f32[]{:T(128)} %get-tuple-element.557), channel_id=1, replica_groups=mesh['gx'=2,'gy'=16] {'gx','gy'}, use_global_device_ids=true, to_apply=%region_1.0 | all-reduce | flops 1 | bytes 8 | tf_op jit(solution)/shard_map/psum | solution.py:101
  61.5 840.4 %while.56 = (s32[]{:T(128)}, f32[16,64,256]{2,1,0:T(8,128)S(1)}, f32[16,15]{0,1:T(8,128)S(1)}, f32[64,256]{1,0:T(8,128)S(1)}, f32[64,256]{1,0:T(8,128)S(1)}, /*i...) while((s32[]{:T(128)}, f32[16,64,256]{2,1,0:T(8,128)S(1)}, ...), condition=%wide.region_7.0_spmd.clone, body=%wide.region_2.7_spmd.clone.sunk | while | flops 7373286 | bytes 4410119 | solution.py:125
  67.7 5.9 collective-permute-done.3
  76.4 37.3 %all-reduce.3 = (f32[16]{0:T(128)S(1)}, f32[]{:T(128)}) all-reduce(f32[16]{0:T(128)S(1)} %convolution_bitcast_fusion.2, f32[]{:T(128)} %get-tuple-element.711), channel_id=1, replica_groups=mesh['gx'=2,'gy'=16] {'gx','gy'}, use_global_device_ids=true, to_apply=%region_3.3 | all-reduce | flops 17 | bytes 136 | tf_op jit(solution)/shard_map/while/body/eval_jaxpr/psum | solution.py:113
  118.5 4.3 collective-permute-start.2
  124.5 5.9 collective-permute-done.3
  133.2 37.1 %all-reduce.3 = (f32[16]{0:T(128)S(1)}, f32[]{:T(128)}) all-reduce(f32[16]{0:T(128)S(1)} %convolution_bitcast_fusion.2, f32[]{:T(128)} %get-tuple-element.711), channel_id=1, replica_groups=mesh['gx'=2,'gy'=16] {'gx','gy'}, use_global_device_ids=true, to_apply=%region_3.3 | all-reduce | flops 17 | bytes 136 | tf_op jit(solution)/shard_map/while/body/eval_jaxpr/psum | solution.py:113
  175.0 3.7 collective-permute-start.2
  180.4 5.9 collective-permute-done.3
  189.2 37.3 %all-reduce.3 = (f32[16]{0:T(128)S(1)}, f32[]{:T(128)}) all-reduce(f32[16]{0:T(128)S(1)} %convolution_bitcast_fusion.2, f32[]{:T(128)} %get-tuple-element.711), channel_id=1, replica_groups=mesh['gx'=2,'gy'=16] {'gx','gy'}, use_global_device_ids=true, to_apply=%region_3.3 | all-reduce | flops 17 | bytes 136 | tf_op jit(solution)/shard_map/while/body/eval_jaxpr/psum | solution.py:113
  231.2 3.7 collective-permute-start.2
  236.5 5.9 collective-permute-done.3
  245.3 37.1 %all-reduce.3 = (f32[16]{0:T(128)S(1)}, f32[]{:T(128)}) all-reduce(f32[16]{0:T(128)S(1)} %convolution_bitcast_fusion.2, f32[]{:T(128)} %get-tuple-element.711), channel_id=1, replica_groups=mesh['gx'=2,'gy'=16] {'gx','gy'}, use_global_device_ids=true, to_apply=%region_3.3 | all-reduce | flops 17 | bytes 136 | tf_op jit(solution)/shard_map/while/body/eval_jaxpr/psum | solution.py:113
  287.1 3.8 collective-permute-start.2
  292.5 5.9 collective-permute-done.3
  301.2 37.3 %all-reduce.3 = (f32[16]{0:T(128)S(1)}, f32[]{:T(128)}) all-reduce(f32[16]{0:T(128)S(1)} %convolution_bitcast_fusion.2, f32[]{:T(128)} %get-tuple-element.711), channel_id=1, replica_groups=mesh['gx'=2,'gy'=16] {'gx','gy'}, use_global_device_ids=true, to_apply=%region_3.3 | all-reduce | flops 17 | bytes 136 | tf_op jit(solution)/shard_map/while/body/eval_jaxpr/psum | solution.py:113
  343.2 3.7 collective-permute-start.2
  348.6 5.9 collective-permute-done.3
  357.3 37.1 %all-reduce.3 = (f32[16]{0:T(128)S(1)}, f32[]{:T(128)}) all-reduce(f32[16]{0:T(128)S(1)} %convolution_bitcast_fusion.2, f32[]{:T(128)} %get-tuple-element.711), channel_id=1, replica_groups=mesh['gx'=2,'gy'=16] {'gx','gy'}, use_global_device_ids=true, to_apply=%region_3.3 | all-reduce | flops 17 | bytes 136 | tf_op jit(solution)/shard_map/while/body/eval_jaxpr/psum | solution.py:113
  399.1 3.8 collective-permute-start.2
  404.5 5.9 collective-permute-done.3
  413.3 37.3 %all-reduce.3 = (f32[16]{0:T(128)S(1)}, f32[]{:T(128)}) all-reduce(f32[16]{0:T(128)S(1)} %convolution_bitcast_fusion.2, f32[]{:T(128)} %get-tuple-element.711), channel_id=1, replica_groups=mesh['gx'=2,'gy'=16] {'gx','gy'}, use_global_device_ids=true, to_apply=%region_3.3 | all-reduce | flops 17 | bytes 136 | tf_op jit(solution)/shard_map/while/body/eval_jaxpr/psum | solution.py:113
  460.6 5.9 collective-permute-done.3
  469.4 37.1 %all-reduce.3 = (f32[16]{0:T(128)S(1)}, f32[]{:T(128)}) all-reduce(f32[16]{0:T(128)S(1)} %convolution_bitcast_fusion.2, f32[]{:T(128)} %get-tuple-element.711), channel_id=1, replica_groups=mesh['gx'=2,'gy'=16] {'gx','gy'}, use_global_device_ids=true, to_apply=%region_3.3 | all-reduce | flops 17 | bytes 136 | tf_op jit(solution)/shard_map/while/body/eval_jaxpr/psum | solution.py:113
  511.1 3.8 collective-permute-start.2
  516.5 5.9 collective-permute-done.3
  525.3 37.3 %all-reduce.3 = (f32[16]{0:T(128)S(1)}, f32[]{:T(128)}) all-reduce(f32[16]{0:T(128)S(1)} %convolution_bitcast_fusion.2, f32[]{:T(128)} %get-tuple-element.711), channel_id=1, replica_groups=mesh['gx'=2,'gy'=16] {'gx','gy'}, use_global_device_ids=true, to_apply=%region_3.3 | all-reduce | flops 17 | bytes 136 | tf_op jit(solution)/shard_map/while/body/eval_jaxpr/psum | solution.py:113
  572.6 5.9 collective-permute-done.3
  581.4 37.1 %all-reduce.3 = (f32[16]{0:T(128)S(1)}, f32[]{:T(128)}) all-reduce(f32[16]{0:T(128)S(1)} %convolution_bitcast_fusion.2, f32[]{:T(128)} %get-tuple-element.711), channel_id=1, replica_groups=mesh['gx'=2,'gy'=16] {'gx','gy'}, use_global_device_ids=true, to_apply=%region_3.3 | all-reduce | flops 17 | bytes 136 | tf_op jit(solution)/shard_map/while/body/eval_jaxpr/psum | solution.py:113
  623.2 3.8 collective-permute-start.2
  628.6 5.9 collective-permute-done.3
  637.4 37.3 %all-reduce.3 = (f32[16]{0:T(128)S(1)}, f32[]{:T(128)}) all-reduce(f32[16]{0:T(128)S(1)} %convolution_bitcast_fusion.2, f32[]{:T(128)} %get-tuple-element.711), channel_id=1, replica_groups=mesh['gx'=2,'gy'=16] {'gx','gy'}, use_global_device_ids=true, to_apply=%region_3.3 | all-reduce | flops 17 | bytes 136 | tf_op jit(solution)/shard_map/while/body/eval_jaxpr/psum | solution.py:113
  684.7 5.9 collective-permute-done.3
  693.4 37.1 %all-reduce.3 = (f32[16]{0:T(128)S(1)}, f32[]{:T(128)}) all-reduce(f32[16]{0:T(128)S(1)} %convolution_bitcast_fusion.2, f32[]{:T(128)} %get-tuple-element.711), channel_id=1, replica_groups=mesh['gx'=2,'gy'=16] {'gx','gy'}, use_global_device_ids=true, to_apply=%region_3.3 | all-reduce | flops 17 | bytes 136 | tf_op jit(solution)/shard_map/while/body/eval_jaxpr/psum | solution.py:113
  735.2 3.8 collective-permute-start.2
  740.6 5.9 collective-permute-done.3
  749.4 37.3 %all-reduce.3 = (f32[16]{0:T(128)S(1)}, f32[]{:T(128)}) all-reduce(f32[16]{0:T(128)S(1)} %convolution_bitcast_fusion.2, f32[]{:T(128)} %get-tuple-element.711), channel_id=1, replica_groups=mesh['gx'=2,'gy'=16] {'gx','gy'}, use_global_device_ids=true, to_apply=%region_3.3 | all-reduce | flops 17 | bytes 136 | tf_op jit(solution)/shard_map/while/body/eval_jaxpr/psum | solution.py:113
  791.4 3.7 collective-permute-start.2
  796.7 5.9 collective-permute-done.3
  805.5 37.1 %all-reduce.3 = (f32[16]{0:T(128)S(1)}, f32[]{:T(128)}) all-reduce(f32[16]{0:T(128)S(1)} %convolution_bitcast_fusion.2, f32[]{:T(128)} %get-tuple-element.711), channel_id=1, replica_groups=mesh['gx'=2,'gy'=16] {'gx','gy'}, use_global_device_ids=true, to_apply=%region_3.3 | all-reduce | flops 17 | bytes 136 | tf_op jit(solution)/shard_map/while/body/eval_jaxpr/psum | solution.py:113
  847.2 3.8 collective-permute-start.2
  852.6 5.9 collective-permute-done.3
  861.4 37.3 %all-reduce.3 = (f32[16]{0:T(128)S(1)}, f32[]{:T(128)}) all-reduce(f32[16]{0:T(128)S(1)} %convolution_bitcast_fusion.2, f32[]{:T(128)} %get-tuple-element.711), channel_id=1, replica_groups=mesh['gx'=2,'gy'=16] {'gx','gy'}, use_global_device_ids=true, to_apply=%region_3.3 | all-reduce | flops 17 | bytes 136 | tf_op jit(solution)/shard_map/while/body/eval_jaxpr/psum | solution.py:113
  902.6 164.1 %while.54 = (s32[]{:T(128)}, f32[16,15]{1,0:T(8,128)S(1)}, f32[16]{0:T(128)S(1)}, s32[]{:T(128)}, s32[2]{0:T(128)S(1)}, /*index=5*/s32[1]{0:T(128)}, s32[]{:T(128)}, s32[]{:T(128)}, s32[]{:T(128)}, s32[]{:T(128)}) while((s32[]{:T(128)}, f32[16,15]{1,0:T(8,128)S(1)}, f32[16]{0:T(128)S(1)}, s32[]{:T(128)}, s32[2]{0:T(128)S(1)}, ...), condition=%wide.region_11.12_spmd, body=%wide.region_8.11_spmd.sunk | while | flops 165 | bytes 5167 | solution.py:81
  1066.6 59.4 %while.55 = (s32[]{:T(128)}, f32[15]{0:T(128)S(1)}, f32[16]{0:T(128)S(1)}, f32[16,15]{1,0:T(8,128)S(1)}, s32[]{:T(128)}, /*index=5*/s32[]{:T(128)}, s32[]{:T(128)}, s32[]{:T(128)}, s32[]{:T(128)}) while((s32[]{:T(128)}, f32[15]{0:T(128)S(1)}, f32[16]{0:T(128)S(1)}, f32[16,15]{1,0:T(8,128)S(1)}, s32[]{:T(128)}, /*index=5*/s32[]{:T(128)}, ...), condition=%wide.region_14.15_spmd, body=%wide.region_12.14_spmd.sunk | while | flops 43 | bytes 490 | solution.py:88
  1134.1 5.9 collective-permute-done.15
  (575 shorter events, 243.5 us)
Async XLA Ops:
  1.4 9.0 collective-permute-start.8
  1.9 8.5 collective-permute-start.9
  3.7 12.5 %collective-permute-start.6 = (f32[68,2]{1,0:T(8,128)S(1)}, f32[68,2]{1,0:T(8,128)S(1)}, u32[]{:S(2)}, u32[]{:S(2)}) collective-permute-start(f32[68,2]{1,0:T(8,128)S(1)} %get-tuple-element.582), channel_id=1, source_target_pairs={{1,0},{2,1},{3,2},{4,3},{5,4},{6,5},{7,6},{8,7},{9,8},{10,9},{11,1... | collective-permute-start | bytes 1640 | tf_op jit(solution)/shard_map/ppermute | solution.py:19
  10.4 8.2 collective-permute-start.7
  10.5 9.8 collective-permute-start.10
  10.6 9.7 collective-permute-start.11
  61.6 1.3 collective-permute-start.1
  63.0 4.6 collective-permute-start.2
  66.0 7.6 collective-permute-start.3
  117.1 1.3 collective-permute-start.1
  118.5 6.0 collective-permute-start.2
  122.8 7.6 collective-permute-start.3
  173.6 1.3 collective-permute-start.1
  175.0 5.4 collective-permute-start.2
  178.8 7.6 collective-permute-start.3
  229.8 1.3 collective-permute-start.1
  231.2 5.3 collective-permute-start.2
  234.9 7.6 collective-permute-start.3
  285.6 1.3 collective-permute-start.1
  287.1 5.4 collective-permute-start.2
  290.8 7.6 collective-permute-start.3
  341.8 1.3 collective-permute-start.1
  343.2 5.3 collective-permute-start.2
  346.9 7.6 collective-permute-start.3
  397.7 1.3 collective-permute-start.1
  399.1 5.4 collective-permute-start.2
  402.9 7.6 collective-permute-start.3
  453.9 1.3 collective-permute-start.1
  455.3 5.3 collective-permute-start.2
  459.0 7.6 collective-permute-start.3
  509.7 1.3 collective-permute-start.1
  511.1 5.4 collective-permute-start.2
  514.9 7.6 collective-permute-start.3
  565.9 1.3 collective-permute-start.1
  567.3 5.3 collective-permute-start.2
  571.0 7.6 collective-permute-start.3
  623.2 5.4 collective-permute-start.2
  626.9 7.6 collective-permute-start.3
  679.3 5.3 collective-permute-start.2
  683.0 7.6 collective-permute-start.3
  735.2 5.4 collective-permute-start.2
  739.0 7.6 collective-permute-start.3
  791.4 5.3 collective-permute-start.2
  795.1 7.6 collective-permute-start.3
  847.2 5.4 collective-permute-start.2
  851.0 7.6 collective-permute-start.3
  1128.8 5.3 collective-permute-start.14
  1132.4 7.6 collective-permute-start.15
  (31 other events, 60.3 us)
where the time goes:
time: 1150 us; the launch traced here: 1140 us
  blocking collectives  596 us (52%)
  loops' own time  151 us (13%)
  waiting for transfers between devices  139 us (12%)
  other arithmetic  84 us (7%)
  starting transfers between devices  82.1 us (7%)
  matrix products  45.4 us (4%)
  local copies, waits for them, and re-layouts  41.8 us (4%)
    psum x15, blocking collectives, arnoldi(): lax.psum((local_projection, jnp.sum(applied * applied)), ('gx', 'gy'))  558 us
    ppermute x36, waiting for transfers between devices, padded_2(): lax.ppermute(tail, axis, [(i, (i + 1) % count) for i in range(ends)])  102 us
    another operation x1, loops' own time, least_squares(): lax.fori_loop(0, columns_total, rotate, (hessenberg, target))  100 us
    ppermute x36, starting transfers between devices, padded_2(): lax.ppermute(head, axis, [((i + 1) % count, i) for i in range(ends)])  73.4 us
    psum x1, blocking collectives, shards(): lax.psum(jnp.sum(start_residual * start_residual), ('gx', 'gy'))  38.4 us
    ppermute x36, waiting for transfers between devices, padded_2(): lax.ppermute(head, axis, [((i + 1) % count, i) for i in range(ends)])  37.2 us
    another operation x46, other arithmetic  30.2 us
    another operation x1, loops' own time, least_squares(): lax.fori_loop(0, columns_total, substitute, jnp.zeros((columns_total,), j...  30.2 us
  transfers between devices with their start and end apart: 72, of which 68 were waited for; matrix products, arithmetic and copies ran while one was open for 0% of the time, Pallas kernels for 0%

commit v1 on v0

v1 whole, which is shorter than its diff:
```python
import functools

import jax
import jax.numpy as jnp
from jax import lax
from jax.experimental import pallas as pl
from jax.experimental.pallas import tpu as pltpu
from jax.sharding import PartitionSpec as P

RESTART = 15
HALO = 2 * (RESTART + 1)
LANES = 128
PAD = 8
CENTRE = 5.5
HALF_WIDTH = 5.2
REFINEMENTS = 3
MESH = pl.DeviceIdType.MESH


def two_sum(a, b):
    total = a + b
    shown = total - a
    return total, (a - (total - shown)) + (b - shown)


def add_pairs(a, b):
    total, rest = two_sum(a[0], b[0])
    return total, rest + (a[1] + b[1])


def split(a):
    scaled = a * 4097.0
    high = scaled - (scaled - a)
    return high, a - high


def two_product(a, b):
    product = a * b
    ah, al = split(a)
    bh, bl = split(b)
    return product, ((ah * bh - product) + ah * bl + al * bh) + al * bl


def tree(items, combine):
    items = list(items)
    while len(items) > 1:
        paired = [combine(items[i], items[i + 1]) for i in range(0, len(items) - 1, 2)]
        items = paired + (items[-1:] if len(items) % 2 else [])
    return items[0]


def rolled(x, shift, axis):
    shift %= x.shape[axis]
    return x if shift == 0 else pltpu.roll(x, shift, axis)


def kernel(
    nx_dev, ny_dev,
    b_ref, x0_ref, re_ref, vx_ref, vy_ref, sol_ref, res_ref,
    pack_r, pack_l, from_l, from_r, other, field, coef, centre, vec, app, acc, gram,
    out_sem, in_sem, gram_out, gram_in,
):
    rows, cols = b_ref.shape
    own_tiles = cols // LANES
    tiles = own_tiles + 1
    all_rows = nx_dev * rows
    n_dev = nx_dev * ny_dev
    gx, gy = lax.axis_index("gx"), lax.axis_index("gy")
    me = gx * ny_dev + gy
    partner = 1 - gx
    right, left = lax.rem(gy + 1, ny_dev), lax.rem(gy + ny_dev - 1, ny_dev)
    inputs = (x0_ref, vx_ref, vy_ref, re_ref, b_ref)
    fold = rows // 4

    def device(step):
        target = lax.rem(me + step, n_dev)
        return target // ny_dev, lax.rem(target, ny_dev)

    barrier = pltpu.get_barrier_semaphore()

    def greet(step, carry):
        pl.semaphore_signal(barrier, inc=1, device_id=device(step), device_id_type=MESH)
        return carry

    lax.fori_loop(1, n_dev, greet, 0)

    lane = lax.broadcasted_iota(jnp.int32, (8, LANES), 1)
    lane_f = lax.broadcasted_iota(jnp.int32, (fold, LANES), 1)

    for pack, tile, base in ((pack_r, own_tiles - 1, LANES - HALO), (pack_l, 0, 0)):
        at = slice(tile * LANES, (tile + 1) * LANES)
        for r in range(0, rows, fold):
            parts = [
                rolled(inputs[f][r:r + fold, at], 32 * f - base, 1) for f in range(4)
            ]
            packed = parts[3]
            for f in (2, 1, 0):
                packed = jnp.where(lane_f < 32 * (f + 1), parts[f], packed)
            pack[r:r + fold, :] = packed
        parts = [rolled(b_ref[q * fold:(q + 1) * fold, at], 32 * q - base, 1) for q in range(4)]
        packed = parts[3]
        for q in (2, 1, 0):
            packed = jnp.where(lane_f < 32 * (q + 1), parts[q], packed)
        pack[rows:rows + fold, :] = packed

    pl.semaphore_wait(barrier, n_dev - 1)

    copies = []

    def send(src, dst, target):
        k = len(copies)
        copy = pltpu.make_async_remote_copy(
            src_ref=src, dst_ref=dst, send_sem=out_sem.at[k], recv_sem=in_sem.at[k],
            device_id=target, device_id_type=MESH,
        )
        copy.start()
        copies.append(copy)

    send(pack_r, from_l.at[0], (gx, right))
    send(pack_l, from_r.at[0], (gx, left))
    send(pack_r, from_l.at[1], (partner, right))
    send(pack_l, from_r.at[1], (partner, left))
    for f in range(5):
        send(inputs[f], other.at[f], (partner, gy))

    for f in range(5):
        for t in range(own_tiles):
            field[f, t, PAD:PAD + rows, :] = inputs[f][:, t * LANES:(t + 1) * LANES]
    for f in range(5):
        copies[4 + f].wait()
        for t in range(own_tiles):
            field[f, t, PAD + rows:PAD + all_rows, :] = other[f, :, t * LANES:(t + 1) * LANES]
    for k in range(4):
        copies[k].wait()
    for h in range(2):
        for f in range(5):
            for r in range(0, rows, fold):
                if f < 4:
                    off = 32 * f
                    at_r, at_l = from_r[h, r:r + fold, :], from_l[h, r:r + fold, :]
                else:
                    off = 32 * (r // fold)
                    at_r, at_l = from_r[h, rows:rows + fold, :], from_l[h, rows:rows + fold, :]
                edge = jnp.where(
                    lane_f < HALO, rolled(at_r, -off, 1),
                    jnp.where(lane_f >= LANES - HALO, rolled(at_l, LANES - HALO - off, 1), 0.0),
                )
                start = PAD + h * rows + r
                field[f, own_tiles, start:start + fold, :] = edge

    def wrap(ref, t):
        ref[t, 0:PAD, :] = ref[t, all_rows:all_rows + PAD, :]
        ref[t, PAD + all_rows:2 * PAD + all_rows, :] = ref[t, PAD:2 * PAD, :]

    for f in range(2):
        for t in range(tiles):
            wrap(field.at[f], t)

    chunk = 16
    lane_c = lax.broadcasted_iota(jnp.int32, (chunk, LANES), 1)

    def along(values, offset):
        shifted = [rolled(v, -offset, 1) for v in values]
        step = 1 if offset > 0 else -1
        keep = lane_c < LANES - offset if offset > 0 else lane_c >= -offset
        return [
            jnp.where(keep, shifted[t], shifted[(t + step) % tiles]) for t in range(tiles)
        ]

    offsets = (-2, -1, 1, 2)
    plain = {-2: 1.0 / 12.0, -1: -4.0 / 3.0, 1: -4.0 / 3.0, 2: 1.0 / 12.0}
    speed = {-2: 1.0 / 24.0, -1: -1.0 / 3.0, 1: 1.0 / 3.0, 2: -1.0 / 24.0}

    for r in range(0, all_rows, chunk):
        here = slice(PAD + r, PAD + r + chunk)
        vy = [field[2, t, here, :] for t in range(tiles)]
        for n, o in enumerate(offsets):
            moved = along(vy, o)
            for t in range(tiles):
                vx = field[1, t, here, :]
                vx_o = field[1, t, PAD + r + o:PAD + r + o + chunk, :]
                coef[n, t, r:r + chunk, :] = plain[o] + speed[o] * (vx + vx_o)
                coef[4 + n, t, r:r + chunk, :] = plain[o] + speed[o] * (vy[t] + moved[t])
        for t in range(tiles):
            centre[t, r:r + chunk, :] = 5.0 + field[3, t, here, :]

    def operate(src, r):
        here = slice(PAD + r, PAD + r + chunk)
        u = [src[t, here, :] for t in range(tiles)]
        total = [centre[t, r:r + chunk, :] * u[t] for t in range(tiles)]
        for n, o in enumerate(offsets):
            moved = along(u, o)
            for t in range(tiles):
                u_o = src[t, PAD + r + o:PAD + r + o + chunk, :]
                total[t] = total[t] + (
                    coef[n, t, r:r + chunk, :] * u_o + coef[4 + n, t, r:r + chunk, :] * moved[t]
                )
        return u, total

    x0 = field.at[0]
    for r in range(0, all_rows, chunk):
        here = slice(PAD + r, PAD + r + chunk)
        _, total = operate(x0, r)
        for t in range(tiles):
            r0 = field[4, t, here, :] - total[t]
            vec[1, t, here, :] = r0
            vec[0, t, here, :] = jnp.zeros_like(r0)
            if r < rows and t < own_tiles:
                app[RESTART, t, r:r + chunk, :] = r0
    for t in range(tiles):
        wrap(vec.at[1], t)

    def step(k, carry):
        src = vec.at[k + 1]
        a = jnp.where(k == 0, 1.0 / HALF_WIDTH, 2.0 / HALF_WIDTH).astype(jnp.float32)
        for r in range(0, all_rows, chunk):
            here = slice(PAD + r, PAD + r + chunk)
            u, total = operate(src, r)
            for t in range(tiles):
                if r < rows and t < own_tiles:
                    app[k, t, r:r + chunk, :] = total[t]
                vec[k + 2, t, here, :] = a * (total[t] - CENTRE * u[t]) - vec[k, t, here, :]
        for t in range(tiles):
            wrap(vec.at[k + 2], t)
        return carry

    lax.fori_loop(0, RESTART, step, 0)

    size = RESTART + 1
    places = [(t, r) for t in range(own_tiles) for r in range(0, rows, 8)]
    for i in range(size):
        mine = [app[i, t, r:r + 8, :] for t, r in places]
        for j in range(i + 1):
            if j == i:
                value = tree([m * m for m in mine], lambda a, b: a + b)
            else:
                value = tree(
                    [m * app[j, t, r:r + 8, :] for m, (t, r) in zip(mine, places)],
                    lambda a, b: a + b,
                )
            for p, q in {(i, j), (j, i)}:
                at = (p * size + q) * 8
                acc[at:at + 8, :] = value

    packed = jnp.zeros((8, LANES), jnp.float32)
    for i in range(size):
        for h in range(2):
            base = (i * size + 8 * h) * 8
            pair = tree(
                [
                    (acc[pl.ds(base + s, 8, stride=8), :], jnp.zeros((8, LANES), jnp.float32))
                    for s in range(8)
                ],
                add_pairs,
            )
            shift = LANES // 2
            while shift:
                pair = add_pairs(pair, tuple(rolled(p, shift, 1) for p in pair))
                shift //= 2
            packed = jnp.where(lane == 32 * h + i, pair[0], packed)
            packed = jnp.where(lane == 32 * h + 16 + i, pair[1], packed)
    gram[me] = packed

    def gram_copy(slot, target):
        return pltpu.make_async_remote_copy(
            src_ref=gram.at[me], dst_ref=gram.at[me], send_sem=gram_out.at[slot],
            recv_sem=gram_in.at[me], device_id=target, device_id_type=MESH,
        )

    def gram_send(step, carry):
        gram_copy(step, device(step)).start()
        return carry

    lax.fori_loop(1, n_dev, gram_send, 0)

    def gram_wait(step, carry):
        source = lax.rem(me + step, n_dev)
        pltpu.make_async_remote_copy(
            src_ref=gram.at[me], dst_ref=gram.at[source], send_sem=gram_out.at[step],
            recv_sem=gram_in.at[source], device_id=device(step), device_id_type=MESH,
        ).wait()
        return carry

    lax.fori_loop(1, n_dev, gram_wait, 0)

    def as_pair(value):
        return (
            jnp.where(lane % 32 < 16, value, 0.0),
            jnp.where(lane % 32 < 16, rolled(value, -16, 1), 0.0),
        )

    total = tree([as_pair(gram[d]) for d in range(n_dev)], add_pairs)

    def unpack(value):
        low = jnp.where(lane < 16, value, 0.0)
        high = jnp.where(lane < 16, rolled(value, -32, 1), 0.0)
        return jnp.concatenate([low, high], axis=0)

    g_high, g_low = unpack(total[0]), unpack(total[1])
    row_g = lax.broadcasted_iota(jnp.int32, (size, LANES), 0)
    lane_g = lax.broadcasted_iota(jnp.int32, (size, LANES), 1)
    m = g_high + jnp.where(lane_g - 16 == row_g, 1.0, 0.0)
    for k in range(RESTART):
        pivot = m[k:k + 1, :] / m[k:k + 1, k:k + 1]
        m = jnp.where(row_g == k, pivot, m - m[:, k:k + 1] * pivot)
    z = jnp.where(row_g < RESTART, jnp.broadcast_to(m[:, RESTART:size], m.shape), -1.0)
    inverse = jnp.where((lane_g < RESTART) & (row_g < RESTART), rolled(m, -16, 1), 0.0)
    for _ in range(REFINEMENTS):
        high, low = two_product(g_high, z)
        low = low + g_low * z
        pair = add_pairs((high[0:8], low[0:8]), (high[8:16], low[8:16]))
        for shift in (4, 2, 1):
            pair = add_pairs(pair, tuple(rolled(p, shift, 0) for p in pair))
        rest = pair[0] + pair[1]
        change = inverse * jnp.concatenate([rest, rest], axis=0)
        z = z - jnp.sum(change, axis=1, keepdims=True)

    weights = [jnp.broadcast_to(z[k:k + 1, :], (8, LANES)) for k in range(RESTART)]
    for t, r in places:
        at = slice(t * LANES, (t + 1) * LANES)
        up = tree(
            [weights[k] * vec[1 + k, t, PAD + r:PAD + r + 8, :] for k in range(RESTART)],
            lambda a, b: a + b,
        )
        sol_ref[r:r + 8, at] = x0_ref[r:r + 8, at] + up
        down = tree(
            [weights[k] * app[k, t, r:r + 8, :] for k in range(RESTART)], lambda a, b: a + b
        )
        res_ref[r:r + 8, at] = app[RESTART, t, r:r + 8, :] - down


def shards(nx_dev, ny_dev, right_side, initial, reaction, velocity_x, velocity_y):
    rows, cols = right_side.shape
    tiles = cols // LANES + 1
    all_rows = nx_dev * rows
    n_dev = nx_dev * ny_dev
    size = RESTART + 1
    padded = all_rows + 2 * PAD
    pack = (rows + rows // 4, LANES)
    f32 = jnp.float32
    out = jax.ShapeDtypeStruct((rows, cols), f32)
    vmem = pl.BlockSpec(memory_space=pltpu.VMEM)
    return pl.pallas_call(
        functools.partial(kernel, nx_dev, ny_dev),
        out_shape=(out, out),
        in_specs=[vmem] * 5,
        out_specs=(vmem, vmem),
        scratch_shapes=[
            pltpu.VMEM(pack, f32),
            pltpu.VMEM(pack, f32),
            pltpu.VMEM((2,) + pack, f32),
            pltpu.VMEM((2,) + pack, f32),
            pltpu.VMEM((5, rows, cols), f32),
            pltpu.VMEM((5, tiles, padded, LANES), f32),
            pltpu.VMEM((8, tiles, all_rows, LANES), f32),
            pltpu.VMEM((tiles, all_rows, LANES), f32),
            pltpu.VMEM((RESTART + 2, tiles, padded, LANES), f32),
            pltpu.VMEM((size, cols // LANES, rows, LANES), f32),
            pltpu.VMEM((size * size * 8, LANES), f32),
            pltpu.VMEM((n_dev, 8, LANES), f32),
            pltpu.SemaphoreType.DMA((9,)),
            pltpu.SemaphoreType.DMA((9,)),
            pltpu.SemaphoreType.DMA((n_dev,)),
            pltpu.SemaphoreType.DMA((n_dev,)),
        ],
        compiler_params=pltpu.CompilerParams(collective_id=0, has_side_effects=True),
        name="gmres_cycle",
    )(right_side, initial, reaction, velocity_x, velocity_y)


def solution(mesh):
    spec = P("gx", "gy")
    return jax.shard_map(
        functools.partial(shards, mesh.shape["gx"], mesh.shape["gy"]),
        mesh=mesh,
        in_specs=(spec,) * 5,
        out_specs=(spec, spec),
        check_vma=False,
    )
```

time: 1150 us -> 31.7 us (0.03)
  blocking collectives: 596 us -> 0 us
  loops' own time: 151 us -> 0 us
  waiting for transfers between devices: 139 us -> 0 us
  other arithmetic: 84 us -> 0 us
  starting transfers between devices: 82.1 us -> 0 us
  matrix products: 45.4 us -> 0 us
  local copies, waits for them, and re-layouts: 41.8 us -> 2.14 us
  Pallas kernels: 0 us -> 28.7 us
    psum x16 -> x0, blocking collectives: 596 us -> none  [the longest x15 558 us: arnoldi(): lax.psum((local_projection, jnp.sum(applied * applied)), ('gx', 'gy'))]
    another operation x3 -> x0, loops' own time: 151 us -> none  [the longest x1 100 us: least_squares(): lax.fori_loop(0, columns_total, rotate, (hessenberg, target))]
    ppermute x72 -> x0, waiting for transfers between devices: 139 us -> none  [the longest x36 102 us: padded_2(): lax.ppermute(tail, axis, [(i, (i + 1) % count) for i in range(ends)])]
    ppermute x72 -> x0, starting transfers between devices: 82.1 us -> none  [the longest x36 73.4 us: padded_2(): lax.ppermute(head, axis, [((i + 1) % count, i) for i in range(ends)])]
    dot_general x31 -> x0, matrix products: 45.4 us -> none  [the longest x15 26.6 us: arnoldi(): jnp.einsum('kxy,xy->k', basis, applied, precision=lax.Precision.HIGHEST)]
    dynamic_slice x60 -> x0, local copies, waits for them, and re-layouts: 36.8 us -> none  [the longest x15 10.1 us: rotate(): diagonal_entry = top_row[column]]
    reduce_sum x46 -> x0, other arithmetic: 32 us -> none  [the longest x15 12.9 us: arnoldi(): jnp.sum(applied * applied)]
    another operation x46 -> x0, other arithmetic: 30.2 us -> none
  transfers between devices with their start and end apart: 72 -> 0, of which waited for: 68 -> 0; matrix products, arithmetic and copies ran while one was open for 0% -> 0% of each run, Pallas kernels for 0% -> 0%
where the time goes in v1:
time: 31.7 us; the launch traced here: 31.5 us
  Pallas kernels  28.7 us (91%)
  local copies, waits for them, and re-layouts  2.14 us (7%)
  between operations  0.65 us (2%)
    pallas_call x1, Pallas kernels, shards(): pl.pallas_call(functools.partial(kernel, nx_dev, ny_dev), out_shape=(out,...  28.7 us
    unnamed x4, local copies, waits for them, and re-layouts  2.14 us

profile of v1, /device:TPU:0, one launch (start us, length us, event | category | flops | bytes accessed | tf_op | source)
XLA Modules:
  0.0 31.5 jit_solution(1028397160115755069)
XLA Ops:
  0.6 28.7 %gmres_cycle.1 = (f32[64,256]{1,0:T(8,128)}, f32[64,256]{1,0:T(8,128)}) custom-call(f32[64,256]{1,0:T(8,128)} %b_ref.1, f32[64,256]{1,0:T(8,128)} %x0_ref.1, f32[64,256]{1,0:T(8,128)} %re_ref.1, f32[64,256]{1,0:T(8,128)} %vx_ref.1, f32[64,256]{1,0:T(8,128)} %vy_ref.1), custom_call_target="tpu_custom_call" | custom-call | tf_op jit(solution)/shard_map/gmres_cycle/pallas_call | solution.py:343
  29.4 0.0 copy-start
  29.4 1.5 %copy.9 = f32[64,256]{1,0:T(8,128)} copy(f32[64,256]{1,0:T(8,128)} %get-tuple-element.4) | data formatting | bytes 131072
  30.9 0.0 copy-done
  30.9 0.6 %copy.10 = f32[64,256]{1,0:T(8,128)} copy(f32[64,256]{1,0:T(8,128)S(1)} %copy-done) | data formatting | bytes 131072
Async XLA Ops:
  29.4 1.5 %copy-start = (f32[64,256]{1,0:T(8,128)S(1)}, f32[64,256]{1,0:T(8,128)}, u32[]{:S(2)}) copy-start(f32[64,256]{1,0:T(8,128)} %get-tuple-element.5) | copy-start | bytes 196612

commit v2 on v1

--- a/solution.py
+++ b/solution.py
@@ -13,7 +13,7 @@
 PAD = 8
 CENTRE = 5.5
 HALF_WIDTH = 5.2
-REFINEMENTS = 3
+REFINEMENTS = 2
 MESH = pl.DeviceIdType.MESH
 
 
@@ -72,17 +72,16 @@
     inputs = (x0_ref, vx_ref, vy_ref, re_ref, b_ref)
     fold = rows // 4
 
-    def device(step):
-        target = lax.rem(me + step, n_dev)
-        return target // ny_dev, lax.rem(target, ny_dev)
-
     barrier = pltpu.get_barrier_semaphore()
 
     def greet(step, carry):
-        pl.semaphore_signal(barrier, inc=1, device_id=device(step), device_id_type=MESH)
+        there = lax.rem(gy + step, ny_dev)
+        for core in (gx, partner):
+            pl.semaphore_signal(barrier, inc=1, device_id=(core, there), device_id_type=MESH)
         return carry
 
-    lax.fori_loop(1, n_dev, greet, 0)
+    pl.semaphore_signal(barrier, inc=1, device_id=(partner, gy), device_id_type=MESH)
+    lax.fori_loop(1, ny_dev, greet, 0)
 
     lane = lax.broadcasted_iota(jnp.int32, (8, LANES), 1)
     lane_f = lax.broadcasted_iota(jnp.int32, (fold, LANES), 1)
@@ -103,6 +102,10 @@
             packed = jnp.where(lane_f < 32 * (q + 1), parts[q], packed)
         pack[rows:rows + fold, :] = packed
 
+    for f in range(5):
+        for t in range(own_tiles):
+            field[f, t, PAD:PAD + rows, :] = inputs[f][:, t * LANES:(t + 1) * LANES]
+
     pl.semaphore_wait(barrier, n_dev - 1)
 
     copies = []
@@ -123,9 +126,6 @@
     for f in range(5):
         send(inputs[f], other.at[f], (partner, gy))
 
-    for f in range(5):
-        for t in range(own_tiles):
-            field[f, t, PAD:PAD + rows, :] = inputs[f][:, t * LANES:(t + 1) * LANES]
     for f in range(5):
         copies[4 + f].wait()
         for t in range(own_tiles):
@@ -259,46 +259,61 @@
                 shift //= 2
             packed = jnp.where(lane == 32 * h + i, pair[0], packed)
             packed = jnp.where(lane == 32 * h + 16 + i, pair[1], packed)
-    gram[me] = packed
-
-    def gram_copy(slot, target):
+    gram[me, 0:4, :] = jnp.where(
+        lane < LANES // 2, packed, rolled(rolled(packed, 4, 0), LANES // 2, 1)
+    )[0:4]
+
+    def gram_copy(core, there):
+        source = core * ny_dev + there
         return pltpu.make_async_remote_copy(
-            src_ref=gram.at[me], dst_ref=gram.at[me], send_sem=gram_out.at[slot],
-            recv_sem=gram_in.at[me], device_id=target, device_id_type=MESH,
+            src_ref=gram.at[me, 0:4], dst_ref=gram.at[me, 0:4], send_sem=gram_out.at[source],
+            recv_sem=gram_in.at[me], device_id=(core, there), device_id_type=MESH,
         )
 
     def gram_send(step, carry):
-        gram_copy(step, device(step)).start()
+        there = lax.rem(gy + step, ny_dev)
+        for core in (gx, partner):
+            gram_copy(core, there).start()
         return carry
 
-    lax.fori_loop(1, n_dev, gram_send, 0)
+    lax.fori_loop(1, ny_dev, gram_send, 0)
+    gram_copy(partner, gy).start()
+
+    def gram_done(core, there):
+        source = core * ny_dev + there
+        pltpu.make_async_remote_copy(
+            src_ref=gram.at[me, 0:4], dst_ref=gram.at[source, 0:4],
+            send_sem=gram_out.at[source], recv_sem=gram_in.at[source],
+            device_id=(core, there), device_id_type=MESH,
+        ).wait()
 
     def gram_wait(step, carry):
-        source = lax.rem(me + step, n_dev)
-        pltpu.make_async_remote_copy(
-            src_ref=gram.at[me], dst_ref=gram.at[source], send_sem=gram_out.at[step],
-            recv_sem=gram_in.at[source], device_id=device(step), device_id_type=MESH,
-        ).wait()
+        there = lax.rem(gy + step, ny_dev)
+        for core in (gx, partner):
+            gram_done(core, there)
         return carry
 
-    lax.fori_loop(1, n_dev, gram_wait, 0)
+    gram_done(partner, gy)
+    lax.fori_loop(1, ny_dev, gram_wait, 0)
+
+    lane_4 = lax.broadcasted_iota(jnp.int32, (4, LANES), 1)
 
     def as_pair(value):
         return (
-            jnp.where(lane % 32 < 16, value, 0.0),
-            jnp.where(lane % 32 < 16, rolled(value, -16, 1), 0.0),
-        )
-
-    total = tree([as_pair(gram[d]) for d in range(n_dev)], add_pairs)
-
-    def unpack(value):
-        low = jnp.where(lane < 16, value, 0.0)
-        high = jnp.where(lane < 16, rolled(value, -32, 1), 0.0)
-        return jnp.concatenate([low, high], axis=0)
-
-    g_high, g_low = unpack(total[0]), unpack(total[1])
+            jnp.where(lane_4 % 32 < 16, value, 0.0),
+            jnp.where(lane_4 % 32 < 16, rolled(value, -16, 1), 0.0),
+        )
+
+    total = tree([as_pair(gram[d, 0:4, :]) for d in range(n_dev)], add_pairs)
+
     row_g = lax.broadcasted_iota(jnp.int32, (size, LANES), 0)
     lane_g = lax.broadcasted_iota(jnp.int32, (size, LANES), 1)
+
+    def unpack(value):
+        quarters = [rolled(value, -shift, 1) for shift in (0, 64, 32, 96)]
+        return jnp.where(lane_g < 16, jnp.concatenate(quarters, axis=0), 0.0)
+
+    g_high, g_low = unpack(total[0]), unpack(total[1])
     m = g_high + jnp.where(lane_g - 16 == row_g, 1.0, 0.0)
     for k in range(RESTART):
         pivot = m[k:k + 1, :] / m[k:k + 1, k:k + 1]
@@ -322,11 +337,11 @@
             [weights[k] * vec[1 + k, t, PAD + r:PAD + r + 8, :] for k in range(RESTART)],
             lambda a, b: a + b,
         )
-        sol_ref[r:r + 8, at] = x0_ref[r:r + 8, at] + up
+        sol_ref[r:r + 8, at] = up
         down = tree(
             [weights[k] * app[k, t, r:r + 8, :] for k in range(RESTART)], lambda a, b: a + b
         )
-        res_ref[r:r + 8, at] = app[RESTART, t, r:r + 8, :] - down
+        res_ref[r:r + 8, at] = (b_ref[r:r + 8, at] - app[RESTART, t, r:r + 8, :]) + down
 
 
 def shards(nx_dev, ny_dev, right_side, initial, reaction, velocity_x, velocity_y):
@@ -340,7 +355,7 @@
     f32 = jnp.float32
     out = jax.ShapeDtypeStruct((rows, cols), f32)
     vmem = pl.BlockSpec(memory_space=pltpu.VMEM)
-    return pl.pallas_call(
+    update, applied = pl.pallas_call(
         functools.partial(kernel, nx_dev, ny_dev),
         out_shape=(out, out),
         in_specs=[vmem] * 5,
@@ -366,6 +381,7 @@
         compiler_params=pltpu.CompilerParams(collective_id=0, has_side_effects=True),
         name="gmres_cycle",
     )(right_side, initial, reaction, velocity_x, velocity_y)
+    return initial + update, right_side - applied
 
 
 def solution(mesh):

time: 31.7 us -> 31 us (0.978)
  other arithmetic: 0 us -> 2.15 us
  local copies, waits for them, and re-layouts: 2.14 us -> 0.01 us
  Pallas kernels: 28.7 us -> 28 us
    unnamed x4 -> x6, local copies, waits for them, and re-layouts: 2.14 us -> 0.01 us
    add x0 -> x1, other arithmetic: none -> 1.51 us  [shards(): return (initial + update, right_side - applied)]
    pallas_call x1, Pallas kernels: 28.7 us -> 28 us  [shards(): pl.pallas_call(functools.partial(kernel, nx_dev, ny_dev), out_shape=(out,...]
    sub x0 -> x1, other arithmetic: none -> 0.64 us  [shards(): return (initial + update, right_side - applied)]
where the time goes in v2:
time: 31 us; the launch traced here: 30.8 us
  Pallas kernels  28 us (90%)
  other arithmetic  2.15 us (7%)
  between operations  0.67 us (2%)
    pallas_call x1, Pallas kernels, shards(): pl.pallas_call(functools.partial(kernel, nx_dev, ny_dev), out_shape=(out,...  28 us
    add x1, other arithmetic, shards(): return (initial + update, right_side - applied)  1.51 us
    sub x1, other arithmetic, shards(): return (initial + update, right_side - applied)  0.64 us

profile of v2, /device:TPU:0, one launch (start us, length us, event | category | flops | bytes accessed | tf_op | source)
XLA Modules:
  0.0 30.8 jit_solution(5737732940624442735)
XLA Ops:
  0.6 0.0 copy-start
  0.6 28.0 %gmres_cycle.1 = (f32[64,256]{1,0:T(8,128)}, f32[64,256]{1,0:T(8,128)}) custom-call(f32[64,256]{1,0:T(8,128)} %b_ref.1, f32[64,256]{1,0:T(8,128)} %x0_ref.1, f32[64,256]{1,0:T(8,128)} %re_ref.1, f32[64,256]{1,0:T(8,128)} %vx_ref.1, f32[64,256]{1,0:T(8,128)} %vy_ref.1), custom_call_target="tpu_custom_call" | custom-call | tf_op jit(solution)/shard_map/gmres_cycle/pallas_call | solution.py:358
  28.6 0.0 copy-done
  28.6 0.0 copy-start.1
  28.7 0.0 copy-start.2
  28.7 1.5 %add.3 = f32[64,256]{1,0:T(8,128)} add(f32[64,256]{1,0:T(8,128)S(1)} %copy-done, f32[64,256]{1,0:T(8,128)} %get-tuple-element.4) | non-fusion elementwise | flops 16384 | bytes 196608 | tf_op jit(solution)/shard_map/add | solution.py:384
  30.2 0.0 copy-done.1
  30.2 0.0 copy-done.2
  30.2 0.6 %sub.3 = f32[64,256]{1,0:T(8,128)} subtract(f32[64,256]{1,0:T(8,128)S(1)} %copy-done.1, f32[64,256]{1,0:T(8,128)S(1)} %copy-done.2) | non-fusion elementwise | flops 16384 | bytes 196608 | tf_op jit(solution)/shard_map/sub | solution.py:384
Async XLA Ops:
  0.6 28.0 %copy-start = (f32[64,256]{1,0:T(8,128)S(1)}, f32[64,256]{1,0:T(8,128)}, u32[]{:S(2)}) copy-start(f32[64,256]{1,0:T(8,128)} %x0_ref.1) | copy-start | bytes 196612
  28.6 1.5 %copy-start.1 = (f32[64,256]{1,0:T(8,128)S(1)}, f32[64,256]{1,0:T(8,128)}, u32[]{:S(2)}) copy-start(f32[64,256]{1,0:T(8,128)} %b_ref.1) | copy-start | bytes 196612
  28.7 1.5 %copy-start.2 = (f32[64,256]{1,0:T(8,128)S(1)}, f32[64,256]{1,0:T(8,128)}, u32[]{:S(2)}) copy-start(f32[64,256]{1,0:T(8,128)} %get-tuple-element.5) | copy-start | bytes 196612
